TPU v7x, 128 devices: a whole 4x4x4 slice. The times are simulated.
128 devices in a mesh: gx: 8 (over z, core), gy: 16 (over x, y).
Axes of the slice: x: 4, y: 4, z: 4, core: 2. Of those that a mesh axis runs over, the one named last changes fastest.
Arguments:
- policy_logp: float32 [16, 2048, 4096], P('gy', 'gx'), may hold values from -2 to 0
- anchor_logp: float32 [16, 2048, 4096], P('gy', 'gx'), may hold values from -2 to 0
- lengths: int32 [16, 2048], P('gy', 'gx'), may hold values from 512 to 4096
- rewards: int32 [16, 2048], P('gy', 'gx'), may hold values from 0 to 8
- slot_prompt: int32 [16, 2048], P('gy', 'gx'), may hold values from 0 to 2047, as said below
Outputs:
- token_grad: float32 [16, 2048, 4096], P(None, ('gx', 'gy'))
- sample_loss: float32 [16, 2048], P(None, ('gx', 'gy'))
- advantage: float32 [16, 2048], P(None, ('gx', 'gy'))
Inputs may be any that keep to these rules, and one draw needn't show every extreme that they name: `slot_prompt`: for every member k and every aligned block of 256 slots, the slots of the block hold each prompt of the same block exactly once.
All inputs are finite; a program needn't handle non-finite values.
Results may differ from a plain program's by a relative error of at most 0.00002.
Values sent between devices are 32-bit elements; how exact they have to be, the bound alone decides.
A program may use at most 64 MiB of HBM per device.

v0:
```python
import jax
import jax.numpy as jnp
from jax import lax
from jax.sharding import Mesh
from jax.sharding import PartitionSpec as P

GX_GY = ("gx_0", "gx_1", "gy_0", "gy_1")
GY = ("gy_0", "gy_1")
GX = ("gx_0", "gx_1")


kl_weight = 0.1


def by_axis(x, axes):
    for axis in axes:
        x = lax.psum(x, axis)
    return x


def sent_together(arrays, axis, split_dim, concat_dim, along):
    columns = [a.reshape(*a.shape[:along], -1) for a in arrays]
    both = jnp.concatenate(columns, axis=along)
    out, at, gathered = (
        lax.all_to_all(both, axis, split_axis=split_dim, concat_axis=concat_dim, tiled=True),
        0,
        [],
    )
    for a, column in zip(arrays, columns):
        piece = out[..., at : at + column.shape[along]]
        gathered.append(piece.reshape(*piece.shape[:along], *a.shape[along:]))
        at += column.shape[along]
    return tuple(gathered)


def score_tokens(policy, anchor, seq_len, reward, total, members, grad_scale, loss_scale):
    advantage = (members * reward - total[None, :]) / (members - 1)
    positions = lax.broadcasted_iota(jnp.float32, policy.shape, 2)
    valid = positions < seq_len[:, :, None]
    log_ratio = anchor - policy
    ratio = jnp.exp(log_ratio)
    token_term = -advantage[:, :, None] * policy + kl_weight * (ratio - log_ratio - 1.0)
    token_grad = (
        jnp.where(valid, -advantage[:, :, None] + kl_weight * (1.0 - ratio), 0.0) * grad_scale
    )
    sample_loss = jnp.sum(jnp.where(valid, token_term, 0.0), axis=2) * loss_scale
    return (token_grad, sample_loss, advantage)


def body(policy_logp, anchor_logp, lengths, rewards, slot_prompt):
    members_dev, slots, seq_slots = policy_logp.shape
    local_prompt = slot_prompt % slots
    member_rows = lax.broadcasted_iota(jnp.int32, (members_dev, slots), 0)
    slot_ids = lax.broadcasted_iota(jnp.int32, (members_dev, slots), 1)
    inverse = jnp.zeros((members_dev, slots), jnp.int32).at[member_rows, local_prompt].set(slot_ids)
    sorted_policy = jnp.take_along_axis(policy_logp, inverse[:, :, None], axis=1)
    sorted_anchor = jnp.take_along_axis(anchor_logp, inverse[:, :, None], axis=1)
    sorted_len = jnp.take_along_axis(lengths, inverse, axis=1).astype(jnp.float32)
    sorted_reward = jnp.take_along_axis(rewards, inverse, axis=1).astype(jnp.float32) * 0.25
    count_local = jnp.sum(lengths.astype(jnp.float32))
    token_total = by_axis(count_local, GX_GY)
    members = members_dev * lax.axis_size(GY)
    samples = members * slots * lax.axis_size(GX)
    grad_scale = samples * seq_slots / token_total
    loss_scale = samples / token_total
    member_sums = jnp.sum(sorted_reward, axis=0)
    total = by_axis(member_sums, GY)
    token_grad, sample_loss, advantage = score_tokens(
        sorted_policy,
        sorted_anchor,
        sorted_len,
        sorted_reward,
        total,
        members,
        grad_scale,
        loss_scale,
    )
    return sent_together((token_grad, sample_loss, advantage), GY, 1, 0, 2)


def solution(mesh):
    torus = Mesh(mesh.devices.reshape(4, 2, 4, 4), ("gx_0", "gx_1", "gy_0", "gy_1"))
    return jax.shard_map(
        body,
        mesh=torus,
        in_specs=(P(GY, GX, None), P(GY, GX, None), P(GY, GX), P(GY, GX), P(GY, GX)),
        out_specs=(P(None, GX_GY, None), P(None, GX_GY), P(None, GX_GY)),
        check_vma=False,
    )
```

profile of v0, /device:TPU:0, one launch (start us, length us, event | category | flops | bytes accessed | tf_op | source)
XLA Modules:
  0.0 137.0 jit_solution(9556072892073195460)
XLA Ops:
  0.6 0.0 copy-start
  0.6 1.3 convert_reduce_fusion
  1.9 12.5 %psum.44 = f32[]{:T(128)} all-reduce(f32[]{:T(128)} %convert_reduce_fusion), channel_id=1, replica_groups=mesh['gx_0'=4,'gx_1'=2,'gy_0'=4,'gy_1'=4] {'gx_0'}, use_global_device_ids=true, to_apply=%region_4.7 | all-reduce | flops 1 | bytes 8 | tf_op jit(solution)/shard_map/psum | solution.py:17
  14.4 3.1 %psum.45 = f32[]{:T(128)} all-reduce(f32[]{:T(128)} %psum.44), channel_id=1, replica_groups=mesh['gx_0'=4,'gx_1'=2,'gy_0'=4,'gy_1'=4] {'gx_1'}, use_global_device_ids=true, to_apply=%region_5.8 | all-reduce | flops 1 | bytes 8 | tf_op jit(solution)/shard_map/psum | solution.py:17
  17.5 0.7 fusion.11
  18.2 1.4 %scatter_custom_fusion = s32[256]{0:T(256)S(1)} fusion(s32[256]{0:T(256)S(1)} %bitcast.61, s32[256]{0:T(256)S(1)} %iota.12, s32[]{:T(128)} %constant.18.clone.1), kind=kCustom, calls=%fused_computation.40 | custom fusion | bytes 1028 | tf_op jit(solution)/shard_map/scatter | solution.py:55
  19.7 0.0 copy-done
  19.7 1.9 %gather_fusion.1 = s32[256]{0:T(256)S(1)} fusion(s32[256]{0:T(256)S(1)} %bitcast.41, s32[1024]{0:T(1024)S(1)} %pad_clamp_fusion.1), kind=kCustom, calls=%fused_computation.2.clone | custom fusion | bytes 3072 | tf_op jit(solution)/shard_map/jit(take_along_axis)/gather | solution.py:59
  21.7 2.0 %gather_fusion = s32[256]{0:T(256)S(1)} fusion(s32[256]{0:T(256)} %bitcast.42, s32[1024]{0:T(1024)S(1)} %pad_clamp_fusion.1), kind=kCustom, calls=%fused_computation.clone | custom fusion | bytes 3072 | tf_op jit(solution)/shard_map/jit(take_along_axis)/gather | solution.py:58
  23.7 11.1 %all-reduce.2 = (f32[]{:T(128)}, f32[256]{0:T(256)S(1)}) all-reduce(f32[]{:T(128)} %psum.45, f32[256]{0:T(256)S(1)} %bitcast.62), channel_id=1, replica_groups=mesh['gx_0'=4,'gx_1'=2,'gy_0'=4,'gy_1'=4] {'gy_0'}, use_global_device_ids=true, to_apply=%region_6.9 | all-reduce | flops 257 | bytes 2056 | tf_op jit(solution)/shard_map/psum | solution.py:17
  34.8 11.3 %all-reduce.1 = (f32[]{:T(128)}, f32[1,256]{1,0:T(1,128)S(1)}) all-reduce(f32[]{:T(128)} %get-tuple-element.9, f32[1,256]{1,0:T(1,128)S(1)} %bitcast.63), channel_id=1, replica_groups=mesh['gx_0'=4,'gx_1'=2,'gy_0'=4,'gy_1'=4] {'gy_1'}, use_global_device_ids=true, to_apply=%region_7.10 | all-reduce | flops 257 | bytes 2056 | tf_op jit(solution)/shard_map/psum | solution.py:17
  47.5 0.1 copy.23
  47.7 7.9 %gather_fusion.3 = f32[256,4096]{1,0:T(8,128)} fusion(f32[256,4096]{1,0:T(8,128)} %bitcast.43, s32[1024]{0:T(1024)S(1)} %pad_clamp_fusion), kind=kCustom, calls=%fused_computation.3.clone | custom fusion | bytes 8389632 | tf_op jit(solution)/shard_map/jit(take_along_axis)/gather | solution.py:56
  55.6 7.8 %gather_fusion.2 = f32[256,4096]{1,0:T(8,128)} fusion(f32[256,4096]{1,0:T(8,128)} %bitcast.44, s32[1024]{0:T(1024)S(1)} %pad_clamp_fusion), kind=kCustom, calls=%fused_computation.1.clone | custom fusion | bytes 8389632 | tf_op jit(solution)/shard_map/jit(take_along_axis)/gather | solution.py:57
  63.4 6.4 %fusion.8 = (f32[256]{0:T(256)S(1)}, f32[1,256,4096]{2,1,0:T(8,128)}) fusion(f32[256,4096]{1,0:T(8,128)} %gather_fusion.3, f32[256,4096]{1,0:T(8,128)} %gather_fusion.2, f32[256]{0:T(256)S(1)} %bitcast.55, f32[256]{0:T(256)S(1)} %bitcast.54, pred[256]{0:T(512)(128)(4,1)S(1)} %get-tuple-element.11, f32[]{:T(128)S(6)} %div.14), kind=kLoop, calls=%fused_computation.15 | loop fusion | flops 16776960 | bytes 12586244 | tf_op jit(solution)/shard_map/reduce_sum | solution.py:46
  69.7 0.1 copy.22
  69.9 5.6 %concatenate.7 = f32[1,256,4098]{2,1,0:T(8,128)} concatenate(f32[1,256,4096]{2,1,0:T(8,128)} %get-tuple-element.16, f32[1,256,1]{2,1,0:T(8,128)S(1)} %copy.22, f32[1,256,1]{2,1,0:T(8,128)S(1)} %copy.23), dimensions={2} | concatenate | bytes 8392704 | tf_op jit(solution)/shard_map/concatenate | solution.py:23
  75.5 6.7 %copy.24 = f32[1,256,4098]{2,0,1:T(1,128)S(1)} copy(f32[1,256,4098]{2,1,0:T(8,128)} %concatenate.7) | data formatting | bytes 8392704 | tf_op jit(solution)/shard_map/concatenate | solution.py:23
  82.1 51.2 %all_to_all.12 = f32[1,256,4098]{2,0,1:T(1,128)S(1)} all-to-all(f32[1,256,4098]{2,0,1:T(1,128)S(1)} %copy.24), channel_id=1, replica_groups=mesh['gx_0'=4,'gx_1'=2,'gy_0'=4,'gy_1'=4] {'gy_0','gy_1'}, dimensions={1} | all-to-all | bytes 8392704 | tf_op jit(solution)/shard_map/all_to_all | solution.py:25
  133.4 0.3 copy.25
  133.7 0.8 slice_reduce_fusion
  134.5 2.5 %slice.24 = f32[16,16,4096]{2,1,0:T(8,128)} slice(f32[16,16,4098]{2,1,0:T(8,128)S(1)} %bitcast.46), slice={[0:16], [0:16], [0:4096]} | slice | bytes 8388608 | tf_op jit(solution)/shard_map/slice | solution.py:30
  (11 shorter events, 0.1 us)
Async XLA Ops:
  0.6 19.1 %copy-start = (s32[1,256]{1,0:T(1,128)S(1)}, s32[1,256]{1,0:T(1,128)}, u32[]{:S(2)}) copy-start(s32[1,256]{1,0:T(1,128)} %param.12) | copy-start | bytes 3076
where the time goes:
time: 138 us; the launch traced here: 137 us
  blocking collectives  89.3 us (65%)
  local copies, waits for them, and re-layouts  37.2 us (27%)
  other arithmetic  8.42 us (6%)
  between operations  2.11 us (2%)
    all_to_all x1, blocking collectives, sent_together(): lax.all_to_all(both, axis, split_axis=split_dim, concat_axis=concat_dim,...  51.2 us
    psum x4, blocking collectives, by_axis(): x = lax.psum(x, axis)  38 us
    concatenate x2, local copies, waits for them, and re-layouts, sent_together(): both = jnp.concatenate(columns, axis=along)  12.2 us
    gather x1, local copies, waits for them, and re-layouts, body(): jnp.take_along_axis(policy_logp, inverse[:, :, None], axis=1)  7.89 us
    gather x1, local copies, waits for them, and re-layouts, body(): jnp.take_along_axis(anchor_logp, inverse[:, :, None], axis=1)  7.8 us
    reduce_sum x1, other arithmetic, score_tokens(): jnp.sum(jnp.where(valid, token_term, 0.0), axis=2) * loss_scale  6.36 us
    slice x2, local copies, waits for them, and re-layouts, sent_together(): piece = out[..., at:at + column.shape[along]]  3.33 us

commit v1 on v0

v1 whole, which is shorter than its diff:
```python
import functools

import jax
import jax.numpy as jnp
from jax import lax
from jax.experimental import pallas as pl
from jax.experimental.pallas import tpu as pltpu
from jax.sharding import Mesh
from jax.sharding import PartitionSpec as P

GX_GY = ("gx_0", "gx_1", "gy_0", "gy_1")
GY = ("gy_0", "gy_1")
GX = ("gx_0", "gx_1")
MESH = pl.DeviceIdType.MESH

MEMBERS = 16
SLOTS = 256
TOKENS = 4096
SAMPLES = 32768
KL = 0.1
CHUNKS = 8
WIDTH = TOKENS // CHUNKS
LANES = 128

OFFSETS = (
    (2, 2), (2, 1), (1, 2), (2, 3), (3, 2), (1, 1), (3, 3), (1, 3),
    (3, 1), (0, 2), (2, 0), (0, 1), (1, 0), (0, 3), (3, 0),
)
GX_OFFSETS = ((2, 1), (2, 0), (1, 1), (3, 1), (1, 0), (3, 0), (0, 1))


def parts_of(x):
    high = x.astype(jnp.bfloat16)
    rest = x - high.astype(jnp.float32)
    mid = rest.astype(jnp.bfloat16)
    low = (rest - mid.astype(jnp.float32)).astype(jnp.bfloat16)
    return high, mid, low


def picked(x, one_hot, contract):
    dims = (((1,), (contract,)), ((), ()))
    high, mid, low = (
        lax.dot_general(part, one_hot, dims, preferred_element_type=jnp.float32)
        for part in parts_of(x)
    )
    return (high + mid) + low


def kernel(
    policy_hbm, anchor_hbm, len_ref, reward_ref, prompt_ref,
    grad_ref, loss_ref, adv_ref,
    policy, anchor, stack, one_hot3, sent, got, sums, len_col,
    info_out, info_in, sums_out, sums_in, count_out, count_in, len_in, adv_in,
    load_sem, send_sem, recv_sem, info_send, info_recv, sums_send, sums_recv, count_send, count_recv,
):
    mz, mc = lax.axis_index("gx_0"), lax.axis_index("gx_1")
    mx, my = lax.axis_index("gy_0"), lax.axis_index("gy_1")
    me = mx * 4 + my
    me_gx = mz * 2 + mc

    def peer(dx, dy):
        return lax.rem(mx + dx, 4), lax.rem(my + dy, 4)

    def loads(ch):
        cols = pl.ds(pl.multiple_of(ch * WIDTH, WIDTH), WIDTH)
        return (
            pltpu.make_async_copy(policy_hbm.at[:, cols], policy.at[:, cols], load_sem.at[0, ch]),
            pltpu.make_async_copy(anchor_hbm.at[:, cols], anchor.at[:, cols], load_sem.at[1, ch]),
        )

    barrier = pltpu.get_barrier_semaphore()
    for dx, dy in OFFSETS:
        px, py = peer(dx, dy)
        pl.semaphore_signal(barrier, inc=1, device_id=(mz, mc, px, py), device_id_type=MESH)
    for dz, dc in GX_OFFSETS:
        pl.semaphore_signal(
            barrier, inc=1, device_id=(lax.rem(mz + dz, 4), lax.rem(mc + dc, 2), mx, my), device_id_type=MESH
        )
    for ch in range(CHUNKS):
        for copy in loads(ch):
            copy.start()

    local_prompt = jnp.bitwise_and(prompt_ref[...], SLOTS - 1)
    rows = lax.broadcasted_iota(jnp.int32, (SLOTS, SLOTS), 0)
    lanes = lax.broadcasted_iota(jnp.int32, (SLOTS, SLOTS), 1)
    hot = jnp.where(rows == local_prompt, 1.0, 0.0).astype(jnp.bfloat16)
    for part in range(3):
        one_hot3[:, part * SLOTS : (part + 1) * SLOTS] = hot
    lens = len_ref[...].astype(jnp.float32)
    rewards = reward_ref[...].astype(jnp.float32) * 0.25
    column = jnp.sum(jnp.where(rows == lanes, lens, 0.0), axis=1, keepdims=True)
    len_col[...] = jnp.broadcast_to(column, (SLOTS, LANES))
    which = lax.broadcasted_iota(jnp.int32, (8, SLOTS), 0)
    both = jnp.where(which == 0, lens, jnp.where(which == 1, rewards, 0.0))
    moved = picked(both, hot, 1)
    local_count = jnp.sum(lens, axis=1, keepdims=True)
    for half in range(2):
        at = half * LANES
        info_out[half, 0:2, :] = moved[0:2, at : at + LANES]
        info_out[half, 2:4, :] = jnp.broadcast_to(local_count, (2, LANES))
    sums[...] = jnp.zeros_like(sums)

    def compute(ch):
        for copy in loads(ch):
            copy.wait()

        @pl.loop(0, SLOTS // 16)
        def _(block):
            r0 = pl.multiple_of(block * 16, 16)
            length = len_col[pl.ds(r0, 16), :]
            s1 = sums[0, pl.ds(r0, 16), :]
            s2 = sums[1, pl.ds(r0, 16), :]
            lane = lax.broadcasted_iota(jnp.int32, (16, LANES), 1)
            for t in range(WIDTH // LANES):
                c0 = pl.multiple_of(ch * WIDTH + t * LANES, LANES)
                p = policy[pl.ds(r0, 16), pl.ds(c0, LANES)]
                a = anchor[pl.ds(r0, 16), pl.ds(c0, LANES)]
                valid = (lane + c0).astype(jnp.float32) < length
                d = a - p
                ratio = jnp.exp(d)
                s1 = s1 + jnp.where(valid, p, 0.0)
                s2 = s2 + jnp.where(valid, ratio - d - 1.0, 0.0)
                for i, part in enumerate(parts_of(ratio)):
                    stack[pl.ds(pl.multiple_of(i * SLOTS + r0, 16), 16), t * LANES : (t + 1) * LANES] = part
            sums[0, pl.ds(r0, 16), :] = s1
            sums[1, pl.ds(r0, 16), :] = s2

        cols = pl.ds(pl.multiple_of(ch * WIDTH, WIDTH), WIDTH)
        sent[:, cols] = jnp.dot(one_hot3[...], stack[...], preferred_element_type=jnp.float32)
        got[me, :, cols] = sent[pl.ds(pl.multiple_of(me * 16, 16), 16), cols]

    def copies(ch):
        cols = pl.ds(pl.multiple_of(ch * WIDTH, WIDTH), WIDTH)
        for j, (dx, dy) in enumerate(OFFSETS):
            px, py = peer(dx, dy)
            first = pl.multiple_of((px * 4 + py) * 16, 16)
            yield pltpu.make_async_remote_copy(
                src_ref=sent.at[pl.ds(first, 16), cols],
                dst_ref=got.at[me, :, cols],
                send_sem=send_sem.at[ch, j],
                recv_sem=recv_sem.at[ch, j],
                device_id=(mz, mc, px, py),
                device_id_type=MESH,
            )

    def small_copies(source, target, sends, recvs):
        for j, (dx, dy) in enumerate(OFFSETS):
            px, py = peer(dx, dy)
            yield pltpu.make_async_remote_copy(
                src_ref=source.at[lax.div(px, 2)],
                dst_ref=target.at[me],
                send_sem=sends.at[j],
                recv_sem=recvs.at[j],
                device_id=(mz, mc, px, py),
                device_id_type=MESH,
            )

    def count_copies():
        for j, (dz, dc) in enumerate(GX_OFFSETS):
            yield pltpu.make_async_remote_copy(
                src_ref=count_out,
                dst_ref=count_in.at[me_gx],
                send_sem=count_send.at[j],
                recv_sem=count_recv.at[j],
                device_id=(lax.rem(mz + dz, 4), lax.rem(mc + dc, 2), mx, my),
                device_id_type=MESH,
            )

    compute(0)
    pl.semaphore_wait(barrier, len(OFFSETS) + len(GX_OFFSETS))
    for copy in small_copies(info_out, info_in, info_send, info_recv):
        copy.start()
    for copy in copies(0):
        copy.start()

    @pl.loop(1, CHUNKS - 1)
    def _(ch):
        compute(ch)
        for copy in copies(ch):
            copy.start()

    compute(CHUNKS - 1)
    ones = jnp.ones((8, LANES), jnp.float32)
    across = (((1,), (1,)), ((), ()))
    row1, row2 = (
        lax.dot_general(ones, sums[i], across, precision=lax.Precision.HIGHEST, preferred_element_type=jnp.float32)
        for i in range(2)
    )
    moved = picked(jnp.where(which == 0, row1, row2), hot, 1)
    for half in range(2):
        at = half * LANES
        sums_out[half] = moved[0:2, at : at + LANES]
    for copy in small_copies(sums_out, sums_in, sums_send, sums_recv):
        copy.start()
    for copy in copies(CHUNKS - 1):
        copy.start()

    half = lax.div(mx, 2)
    info_in[me] = info_out[half]
    sums_in[me] = sums_out[half]
    for copy in small_copies(info_out, info_in, info_send, info_recv):
        copy.wait()
    count = info_in[0, 2:3, :]
    for k in range(1, MEMBERS):
        count = count + info_in[k, 2:3, :]
    count_out[...] = count
    count_in[me_gx] = count
    for copy in count_copies():
        copy.start()

    total = info_in[0, 1:2, :]
    for k in range(1, MEMBERS):
        total = total + info_in[k, 1:2, :]
    lane = lax.broadcasted_iota(jnp.int32, (16, LANES), 1)
    row = lax.broadcasted_iota(jnp.int32, (16, LANES), 0)
    mine = lane == lax.rem(me, 8) * 16 + row

    def to_column(line):
        return jnp.broadcast_to(jnp.sum(jnp.where(mine, line, 0.0), axis=1, keepdims=True), (16, LANES))

    for k in range(MEMBERS):
        advantage = (MEMBERS * info_in[k, 1:2, :] - total) / (MEMBERS - 1)
        len_in[k] = to_column(info_in[k, 0:1, :])
        adv_in[k] = to_column(advantage)

    for copy in count_copies():
        copy.wait()
    tokens = count_in[0]
    for g in range(1, 8):
        tokens = tokens + count_in[g]
    grad_scale = SAMPLES * TOKENS / tokens
    loss_scale = SAMPLES / tokens

    @pl.loop(0, CHUNKS)
    def _(ch):
        for copy in copies(ch):
            copy.wait_recv()

        @pl.loop(0, MEMBERS)
        def _(k):
            length = len_in[k]
            advantage = adv_in[k]
            for t in range(WIDTH // LANES):
                c0 = pl.multiple_of(ch * WIDTH + t * LANES, LANES)
                ratio = got[k, :, pl.ds(c0, LANES)]
                valid = (lane + c0).astype(jnp.float32) < length
                grad_ref[k, :, pl.ds(c0, LANES)] = (
                    jnp.where(valid, KL * (1.0 - ratio) - advantage, 0.0) * grad_scale
                )

    for copy in small_copies(sums_out, sums_in, sums_send, sums_recv):
        copy.wait()
    member = lax.broadcasted_iota(jnp.int32, (MEMBERS, LANES), 0)
    adv_rows = jnp.zeros((MEMBERS, LANES), jnp.float32)
    loss_rows = jnp.zeros((MEMBERS, LANES), jnp.float32)
    for k in range(MEMBERS):
        advantage = (MEMBERS * info_in[k, 1:2, :] - total) / (MEMBERS - 1)
        loss = (KL * sums_in[k, 1:2, :] - advantage * sums_in[k, 0:1, :]) * loss_scale
        adv_rows = jnp.where(member == k, advantage, adv_rows)
        loss_rows = jnp.where(member == k, loss, loss_rows)
    select = jnp.where(mine, 1.0, 0.0).astype(jnp.bfloat16)
    loss_ref[...] = picked(loss_rows, select, 1)
    adv_ref[...] = picked(adv_rows, select, 1)

    @pl.loop(0, CHUNKS)
    def _(ch):
        for copy in copies(ch):
            copy.wait_send()


def body(policy_logp, anchor_logp, lengths, rewards, slot_prompt):
    f32, bf16, dma = jnp.float32, jnp.bfloat16, pltpu.SemaphoreType.DMA
    n = len(OFFSETS)
    vmem = pl.BlockSpec(memory_space=pltpu.VMEM)
    hbm = pl.BlockSpec(memory_space=pl.ANY)
    return pl.pallas_call(
        kernel,
        out_shape=(
            pltpu.VMEM((MEMBERS, 16, TOKENS), f32),
            pltpu.VMEM((MEMBERS, 16), f32),
            pltpu.VMEM((MEMBERS, 16), f32),
        ),
        in_specs=[hbm, hbm, vmem, vmem, vmem],
        out_specs=(vmem, vmem, vmem),
        scratch_shapes=[
            pltpu.VMEM((SLOTS, TOKENS), f32),
            pltpu.VMEM((SLOTS, TOKENS), f32),
            pltpu.VMEM((3 * SLOTS, WIDTH), bf16),
            pltpu.VMEM((SLOTS, 3 * SLOTS), bf16),
            pltpu.VMEM((SLOTS, TOKENS), f32),
            pltpu.VMEM((MEMBERS, 16, TOKENS), f32),
            pltpu.VMEM((2, SLOTS, LANES), f32),
            pltpu.VMEM((SLOTS, LANES), f32),
            pltpu.VMEM((2, 4, LANES), f32),
            pltpu.VMEM((MEMBERS, 4, LANES), f32),
            pltpu.VMEM((2, 2, LANES), f32),
            pltpu.VMEM((MEMBERS, 2, LANES), f32),
            pltpu.VMEM((1, LANES), f32),
            pltpu.VMEM((8, 1, LANES), f32),
            pltpu.VMEM((MEMBERS, 16, LANES), f32),
            pltpu.VMEM((MEMBERS, 16, LANES), f32),
            dma((2, CHUNKS)), dma((CHUNKS, n)), dma((CHUNKS, n)),
            dma((n,)), dma((n,)), dma((n,)), dma((n,)),
            dma((len(GX_OFFSETS),)), dma((len(GX_OFFSETS),)),
        ],
        compiler_params=pltpu.CompilerParams(
            collective_id=0, has_side_effects=True, vmem_limit_bytes=50 * 2**20
        ),
    )(policy_logp.reshape(SLOTS, TOKENS), anchor_logp.reshape(SLOTS, TOKENS), lengths, rewards, slot_prompt)


def solution(mesh):
    torus = Mesh(mesh.devices.reshape(4, 2, 4, 4), ("gx_0", "gx_1", "gy_0", "gy_1"))
    return jax.shard_map(
        body,
        mesh=torus,
        in_specs=(P(GY, GX, None), P(GY, GX, None), P(GY, GX), P(GY, GX), P(GY, GX)),
        out_specs=(P(None, GX_GY, None), P(None, GX_GY), P(None, GX_GY)),
        check_vma=False,
    )
```

time: 138 us -> 62.7 us (0.45)
  blocking collectives: 89.3 us -> 0 us
  Pallas kernels: 0 us -> 58.8 us
  local copies, waits for them, and re-layouts: 37.2 us -> 3.21 us
  other arithmetic: 8.42 us -> 0 us
  between operations: 2.11 us -> 0.64 us
    pallas_call x0 -> x1, Pallas kernels: none -> 58.8 us  [body(): pl.pallas_call(kernel, out_shape=(pltpu.VMEM((MEMBERS, 16, TOKENS), f32),...]
    all_to_all x1 -> x0, blocking collectives: 51.2 us -> none  [sent_together(): lax.all_to_all(both, axis, split_axis=split_dim, concat_axis=concat_dim,...]
    psum x4 -> x0, blocking collectives: 38 us -> none  [by_axis(): x = lax.psum(x, axis)]
    gather x4 -> x0, local copies, waits for them, and re-layouts: 19.6 us -> none  [the longest x1 7.89 us: body(): jnp.take_along_axis(policy_logp, inverse[:, :, None], axis=1)]
    concatenate x3 -> x0, local copies, waits for them, and re-layouts: 12.2 us -> none  [the longest x2 12.2 us: sent_together(): both = jnp.concatenate(columns, axis=along)]
    reduce_sum x2 -> x0, other arithmetic: 7.65 us -> none  [the longest x1 6.36 us: score_tokens(): jnp.sum(jnp.where(valid, token_term, 0.0), axis=2) * loss_scale]
    slice x2 -> x0, local copies, waits for them, and re-layouts: 3.33 us -> none  [sent_together(): piece = out[..., at:at + column.shape[along]]]
    unnamed x3, local copies, waits for them, and re-layouts: 0.29 us -> 3.21 us
where the time goes in v1:
time: 62.7 us; the launch traced here: 62.6 us
  Pallas kernels  58.8 us (94%)
  local copies, waits for them, and re-layouts  3.21 us (5%)
  between operations  0.64 us (1%)
    pallas_call x1, Pallas kernels, body(): pl.pallas_call(kernel, out_shape=(pltpu.VMEM((MEMBERS, 16, TOKENS), f32),...  58.8 us
    unnamed x3, local copies, waits for them, and re-layouts  3.21 us

profile of v1, /device:TPU:0, one launch (start us, length us, event | category | flops | bytes accessed | tf_op | source)
XLA Modules:
  0.0 62.6 jit_solution(10763115354964970299)
XLA Ops:
  0.6 58.8 %shard_map.76 = (f32[16,16,4096]{2,1,0:T(8,128)S(1)}, f32[16,16]{1,0:T(8,128)S(1)}, f32[16,16]{1,0:T(8,128)S(1)}) custom-call(f32[256,4096]{1,0:T(8,128)} %bitcast.2, f32[256,4096]{1,0:T(8,128)} %bitcast.3, s32[1,256]{1,0:T(1,128)} %len_ref.1, s32[1,256]{1,0:T(1,128)} %reward_ref.1, s32[1,256]{1,0:T(1,128)} %prompt_ref.1), custom_call_target="tpu_custom_call" | custom-call | tf_op jit(solution)/shard_map/pallas_call | solution.py:276
  59.4 2.0 %copy.11 = f32[16,16,4096]{2,1,0:T(8,128)} copy(f32[16,16,4096]{2,1,0:T(8,128)S(1)} %get-tuple-element.3) | data formatting | bytes 8388608
  61.4 0.6 copy.12
  62.0 0.6 copy.13

commit v2 on v1

v2 whole, which is shorter than its diff:
```python
import functools

import jax
import jax.numpy as jnp
from jax import lax
from jax.experimental import pallas as pl
from jax.experimental.pallas import tpu as pltpu
from jax.sharding import Mesh
from jax.sharding import PartitionSpec as P

GX_GY = ("gx_0", "gx_1", "gy_0", "gy_1")
GY = ("gy_0", "gy_1")
GX = ("gx_0", "gx_1")
MESH = pl.DeviceIdType.MESH

MEMBERS = 16
SLOTS = 256
TOKENS = 4096
SAMPLES = 32768
KL = 0.1
LANES = 128
UNIT = 256
WIDTHS = (256, 512, 768, 1024, 1024, 512)
STARTS = tuple(sum(WIDTHS[:i]) for i in range(len(WIDTHS)))
CHUNKS = len(WIDTHS)

OFFSETS = (
    (2, 2), (2, 1), (1, 2), (2, 3), (3, 2), (1, 1), (3, 3), (1, 3),
    (3, 1), (0, 2), (2, 0), (0, 1), (1, 0), (0, 3), (3, 0),
)
GX_OFFSETS = ((2, 1), (2, 0), (1, 1), (3, 1), (1, 0), (3, 0), (0, 1))


def parts_of(x):
    high = x.astype(jnp.bfloat16)
    rest = x - high.astype(jnp.float32)
    mid = rest.astype(jnp.bfloat16)
    low = (rest - mid.astype(jnp.float32)).astype(jnp.bfloat16)
    return high, mid, low


def picked(x, one_hot, contract):
    dims = (((1,), (contract,)), ((), ()))
    high, mid, low = (
        lax.dot_general(part, one_hot, dims, preferred_element_type=jnp.float32)
        for part in parts_of(x)
    )
    return (high + mid) + low


def kernel(
    policy_hbm, anchor_hbm, len_hbm, reward_hbm, prompt_hbm,
    grad_ref, loss_ref, adv_ref,
    policy, anchor, facts, stack, one_hot3, sent, got, sums, len_col,
    info_out, info_in, sums_out, sums_in, count_out, count_in, len_in, adv_in,
    load_sem, facts_sem, send_sem, recv_sem,
    info_send, info_recv, sums_send, sums_recv, count_send, count_recv,
):
    mz, mc = lax.axis_index("gx_0"), lax.axis_index("gx_1")
    mx, my = lax.axis_index("gy_0"), lax.axis_index("gy_1")
    me = mx * 4 + my
    me_gx = mz * 2 + mc

    def peer(dx, dy):
        return lax.rem(mx + dx, 4), lax.rem(my + dy, 4)

    def columns(ch):
        return pl.ds(STARTS[ch], WIDTHS[ch])

    def loads(ch):
        cols = columns(ch)
        return (
            pltpu.make_async_copy(policy_hbm.at[:, cols], policy.at[:, cols], load_sem.at[0, ch]),
            pltpu.make_async_copy(anchor_hbm.at[:, cols], anchor.at[:, cols], load_sem.at[1, ch]),
        )

    fact_loads = [
        pltpu.make_async_copy(source, facts.at[i], facts_sem.at[i])
        for i, source in enumerate((prompt_hbm, len_hbm, reward_hbm))
    ]

    barrier = pltpu.get_barrier_semaphore()
    for dx, dy in OFFSETS:
        px, py = peer(dx, dy)
        pl.semaphore_signal(barrier, inc=1, device_id=(mz, mc, px, py), device_id_type=MESH)
    for dz, dc in GX_OFFSETS:
        pl.semaphore_signal(
            barrier, inc=1, device_id=(lax.rem(mz + dz, 4), lax.rem(mc + dc, 2), mx, my), device_id_type=MESH
        )
    for copy in fact_loads:
        copy.start()
    for ch in range(CHUNKS):
        for copy in loads(ch):
            copy.start()
    for copy in fact_loads:
        copy.wait()

    local_prompt = jnp.bitwise_and(facts[0], SLOTS - 1)
    rows = lax.broadcasted_iota(jnp.int32, (SLOTS, SLOTS), 0)
    lanes = lax.broadcasted_iota(jnp.int32, (SLOTS, SLOTS), 1)
    hot = jnp.where(rows == local_prompt, 1.0, 0.0).astype(jnp.bfloat16)
    for part in range(3):
        one_hot3[:, part * SLOTS : (part + 1) * SLOTS] = hot
    lens = facts[1].astype(jnp.float32)
    column = jnp.sum(jnp.where(rows == lanes, lens, 0.0), axis=1, keepdims=True)
    len_col[...] = jnp.broadcast_to(column, (SLOTS, LANES))
    sums[...] = jnp.zeros_like(sums)

    def compute(ch):
        for copy in loads(ch):
            copy.wait()

        @pl.loop(0, WIDTHS[ch] // UNIT)
        def _(unit):
            start = pl.multiple_of(STARTS[ch] + unit * UNIT, UNIT)

            @pl.loop(0, SLOTS // 16)
            def _(block):
                r0 = pl.multiple_of(block * 16, 16)
                length = len_col[pl.ds(r0, 16), :]
                s1 = sums[0, pl.ds(r0, 16), :]
                s2 = sums[1, pl.ds(r0, 16), :]
                lane = lax.broadcasted_iota(jnp.int32, (16, LANES), 1)
                for t in range(UNIT // LANES):
                    c0 = pl.multiple_of(start + t * LANES, LANES)
                    p = policy[pl.ds(r0, 16), pl.ds(c0, LANES)]
                    a = anchor[pl.ds(r0, 16), pl.ds(c0, LANES)]
                    valid = (lane + c0).astype(jnp.float32) < length
                    d = a - p
                    ratio = jnp.exp(d)
                    s1 = s1 + jnp.where(valid, p, 0.0)
                    s2 = s2 + jnp.where(valid, ratio - d - 1.0, 0.0)
                    for i, part in enumerate(parts_of(ratio)):
                        stack[pl.ds(pl.multiple_of(i * SLOTS + r0, 16), 16), t * LANES : (t + 1) * LANES] = part
                sums[0, pl.ds(r0, 16), :] = s1
                sums[1, pl.ds(r0, 16), :] = s2

            cols = pl.ds(start, UNIT)
            sent[:, cols] = jnp.dot(one_hot3[...], stack[...], preferred_element_type=jnp.float32)
            got[me, :, cols] = sent[pl.ds(pl.multiple_of(me * 16, 16), 16), cols]

    def copies(ch):
        for j, (dx, dy) in enumerate(OFFSETS):
            px, py = peer(dx, dy)
            first = pl.multiple_of((px * 4 + py) * 16, 16)
            yield pltpu.make_async_remote_copy(
                src_ref=sent.at[pl.ds(first, 16), columns(ch)],
                dst_ref=got.at[me, :, columns(ch)],
                send_sem=send_sem.at[ch, j],
                recv_sem=recv_sem.at[ch, j],
                device_id=(mz, mc, px, py),
                device_id_type=MESH,
            )

    def small_copies(source, target, sends, recvs):
        for j, (dx, dy) in enumerate(OFFSETS):
            px, py = peer(dx, dy)
            yield pltpu.make_async_remote_copy(
                src_ref=source.at[lax.div(px, 2)],
                dst_ref=target.at[me],
                send_sem=sends.at[j],
                recv_sem=recvs.at[j],
                device_id=(mz, mc, px, py),
                device_id_type=MESH,
            )

    def count_copies():
        for j, (dz, dc) in enumerate(GX_OFFSETS):
            yield pltpu.make_async_remote_copy(
                src_ref=count_out,
                dst_ref=count_in.at[me_gx],
                send_sem=count_send.at[j],
                recv_sem=count_recv.at[j],
                device_id=(lax.rem(mz + dz, 4), lax.rem(mc + dc, 2), mx, my),
                device_id_type=MESH,
            )

    compute(0)
    pl.semaphore_wait(barrier, len(OFFSETS) + len(GX_OFFSETS))
    for copy in copies(0):
        copy.start()

    hot = one_hot3[:, 0:SLOTS]
    lens = facts[1].astype(jnp.float32)
    rewards = facts[2].astype(jnp.float32) * 0.25
    which = lax.broadcasted_iota(jnp.int32, (8, SLOTS), 0)
    both = jnp.where(which == 0, lens, jnp.where(which == 1, rewards, 0.0))
    moved = picked(both, hot, 1)
    local_count = jnp.sum(lens, axis=1, keepdims=True)
    for half in range(2):
        at = half * LANES
        info_out[half, 0:2, :] = moved[0:2, at : at + LANES]
        info_out[half, 2:4, :] = jnp.broadcast_to(local_count, (2, LANES))

    compute(1)
    for copy in small_copies(info_out, info_in, info_send, info_recv):
        copy.start()
    for copy in copies(1):
        copy.start()
    for ch in range(2, CHUNKS):
        compute(ch)
        if ch == CHUNKS - 1:
            ones = jnp.ones((8, LANES), jnp.float32)
            across = (((1,), (1,)), ((), ()))
            row1, row2 = (
                lax.dot_general(
                    ones, sums[i], across, precision=lax.Precision.HIGHEST, preferred_element_type=jnp.float32
                )
                for i in range(2)
            )
            moved = picked(jnp.where(which == 0, row1, row2), hot, 1)
            for half in range(2):
                at = half * LANES
                sums_out[half] = moved[0:2, at : at + LANES]
            for copy in small_copies(sums_out, sums_in, sums_send, sums_recv):
                copy.start()
        for copy in copies(ch):
            copy.start()

    half = lax.div(mx, 2)
    info_in[me] = info_out[half]
    sums_in[me] = sums_out[half]
    for copy in small_copies(info_out, info_in, info_send, info_recv):
        copy.wait()
    count = info_in[0, 2:3, :]
    for k in range(1, MEMBERS):
        count = count + info_in[k, 2:3, :]
    count_out[...] = count
    count_in[me_gx] = count
    for copy in count_copies():
        copy.start()

    total = info_in[0, 1:2, :]
    for k in range(1, MEMBERS):
        total = total + info_in[k, 1:2, :]
    lane = lax.broadcasted_iota(jnp.int32, (16, LANES), 1)
    row = lax.broadcasted_iota(jnp.int32, (16, LANES), 0)
    mine = lane == lax.rem(me, 8) * 16 + row

    def to_column(line):
        return jnp.broadcast_to(jnp.sum(jnp.where(mine, line, 0.0), axis=1, keepdims=True), (16, LANES))

    for k in range(MEMBERS):
        advantage = (MEMBERS * info_in[k, 1:2, :] - total) / (MEMBERS - 1)
        len_in[k] = to_column(info_in[k, 0:1, :])
        adv_in[k] = to_column(advantage)

    for copy in count_copies():
        copy.wait()
    tokens = count_in[0]
    for g in range(1, 8):
        tokens = tokens + count_in[g]
    grad_scale = SAMPLES * TOKENS / tokens
    loss_scale = SAMPLES / tokens

    for ch in range(CHUNKS):
        if ch == CHUNKS - 1:
            for copy in small_copies(sums_out, sums_in, sums_send, sums_recv):
                copy.wait()
            member = lax.broadcasted_iota(jnp.int32, (MEMBERS, LANES), 0)
            adv_rows = jnp.zeros((MEMBERS, LANES), jnp.float32)
            loss_rows = jnp.zeros((MEMBERS, LANES), jnp.float32)
            for k in range(MEMBERS):
                advantage = (MEMBERS * info_in[k, 1:2, :] - total) / (MEMBERS - 1)
                loss = (KL * sums_in[k, 1:2, :] - advantage * sums_in[k, 0:1, :]) * loss_scale
                adv_rows = jnp.where(member == k, advantage, adv_rows)
                loss_rows = jnp.where(member == k, loss, loss_rows)
            select = jnp.where(mine, 1.0, 0.0).astype(jnp.bfloat16)
            loss_ref[...] = picked(loss_rows, select, 1)
            adv_ref[...] = picked(adv_rows, select, 1)
            for earlier in range(CHUNKS - 1):
                for copy in copies(earlier):
                    copy.wait_send()
        for copy in copies(ch):
            copy.wait_recv()

        @pl.loop(0, MEMBERS)
        def _(k):
            length = len_in[k]
            advantage = adv_in[k]
            for t in range(WIDTHS[ch] // LANES):
                c0 = STARTS[ch] + t * LANES
                ratio = got[k, :, c0 : c0 + LANES]
                valid = (lane + c0).astype(jnp.float32) < length
                grad_ref[k, :, c0 : c0 + LANES] = (
                    jnp.where(valid, KL * (1.0 - ratio) - advantage, 0.0) * grad_scale
                )

    for copy in copies(CHUNKS - 1):
        copy.wait_send()


def put_out(grad, loss, adv, grad_out, loss_out, adv_out, sem):
    moves = [
        pltpu.make_async_copy(source, target, sem.at[i])
        for i, (source, target) in enumerate(((loss, loss_out), (adv, adv_out)))
    ]
    pieces = 4
    each = MEMBERS // pieces
    for i in range(pieces):
        part = pl.ds(i * each, each)
        moves.append(pltpu.make_async_copy(grad.at[part], grad_out.at[part], sem.at[2 + i]))
    for move in moves:
        move.start()
    for move in moves:
        move.wait()


def body(policy_logp, anchor_logp, lengths, rewards, slot_prompt):
    f32, bf16, dma = jnp.float32, jnp.bfloat16, pltpu.SemaphoreType.DMA
    n = len(OFFSETS)
    vmem = pl.BlockSpec(memory_space=pltpu.VMEM)
    hbm = pl.BlockSpec(memory_space=pl.ANY)
    results = pl.pallas_call(
        kernel,
        out_shape=(
            pltpu.VMEM((MEMBERS, 16, TOKENS), f32),
            pltpu.VMEM((MEMBERS, 16), f32),
            pltpu.VMEM((MEMBERS, 16), f32),
        ),
        in_specs=[hbm] * 5,
        out_specs=(vmem, vmem, vmem),
        scratch_shapes=[
            pltpu.VMEM((SLOTS, TOKENS), f32),
            pltpu.VMEM((SLOTS, TOKENS), f32),
            pltpu.VMEM((3, 1, SLOTS), jnp.int32),
            pltpu.VMEM((3 * SLOTS, UNIT), bf16),
            pltpu.VMEM((SLOTS, 3 * SLOTS), bf16),
            pltpu.VMEM((SLOTS, TOKENS), f32),
            pltpu.VMEM((MEMBERS, 16, TOKENS), f32),
            pltpu.VMEM((2, SLOTS, LANES), f32),
            pltpu.VMEM((SLOTS, LANES), f32),
            pltpu.VMEM((2, 4, LANES), f32),
            pltpu.VMEM((MEMBERS, 4, LANES), f32),
            pltpu.VMEM((2, 2, LANES), f32),
            pltpu.VMEM((MEMBERS, 2, LANES), f32),
            pltpu.VMEM((1, LANES), f32),
            pltpu.VMEM((8, 1, LANES), f32),
            pltpu.VMEM((MEMBERS, 16, LANES), f32),
            pltpu.VMEM((MEMBERS, 16, LANES), f32),
            dma((2, CHUNKS)), dma((3,)), dma((CHUNKS, n)), dma((CHUNKS, n)),
            dma((n,)), dma((n,)), dma((n,)), dma((n,)),
            dma((len(GX_OFFSETS),)), dma((len(GX_OFFSETS),)),
        ],
        compiler_params=pltpu.CompilerParams(
            collective_id=0, has_side_effects=True, vmem_limit_bytes=50 * 2**20
        ),
    )(policy_logp.reshape(SLOTS, TOKENS), anchor_logp.reshape(SLOTS, TOKENS), lengths, rewards, slot_prompt)
    return pl.pallas_call(
        put_out,
        out_shape=(
            jax.ShapeDtypeStruct((MEMBERS, 16, TOKENS), f32),
            jax.ShapeDtypeStruct((MEMBERS, 16), f32),
            jax.ShapeDtypeStruct((MEMBERS, 16), f32),
        ),
        in_specs=[vmem] * 3,
        out_specs=(hbm, hbm, hbm),
        scratch_shapes=[dma((6,))],
        compiler_params=pltpu.CompilerParams(vmem_limit_bytes=2**20),
    )(*(pltpu.with_memory_space_constraint(r, pltpu.VMEM) for r in results))


def solution(mesh):
    torus = Mesh(mesh.devices.reshape(4, 2, 4, 4), ("gx_0", "gx_1", "gy_0", "gy_1"))
    return jax.shard_map(
        body,
        mesh=torus,
        in_specs=(P(GY, GX, None), P(GY, GX, None), P(GY, GX), P(GY, GX), P(GY, GX)),
        out_specs=(P(None, GX_GY, None), P(None, GX_GY), P(None, GX_GY)),
        check_vma=False,
    )
```

time: 62.7 us -> 60.2 us (0.960)
  local copies, waits for them, and re-layouts: 3.21 us -> 0 us
  Pallas kernels: 58.8 us -> 59.5 us
    unnamed x3 -> x0, local copies, waits for them, and re-layouts: 3.21 us -> none
    pallas_call x0 -> x1, Pallas kernels: none -> 2.07 us  [body(): pl.pallas_call(put_out, out_shape=(jax.ShapeDtypeStruct((MEMBERS, 16, TOK...]
    pallas_call x1, Pallas kernels: 58.8 us -> 57.4 us  [body(): pl.pallas_call(kernel, out_shape=(pltpu.VMEM((MEMBERS, 16, TOKENS), f32),...]
where the time goes in v2:
time: 60.2 us; the launch traced here: 60.1 us
  Pallas kernels  59.5 us (99%)
  between operations  0.64 us (1%)
    pallas_call x1, Pallas kernels, body(): pl.pallas_call(kernel, out_shape=(pltpu.VMEM((MEMBERS, 16, TOKENS), f32),...  57.4 us
    pallas_call x1, Pallas kernels, body(): pl.pallas_call(put_out, out_shape=(jax.ShapeDtypeStruct((MEMBERS, 16, TOK...  2.07 us

profile of v2, /device:TPU:0, one launch (start us, length us, event | category | flops | bytes accessed | tf_op | source)
XLA Modules:
  0.0 60.1 jit_solution(504377471349878112)
XLA Ops:
  0.6 57.4 %shard_map.76 = (f32[16,16,4096]{2,1,0:T(8,128)S(1)}, f32[16,16]{1,0:T(8,128)S(1)}, f32[16,16]{1,0:T(8,128)S(1)}) custom-call(f32[256,4096]{1,0:T(8,128)} %bitcast.2, f32[256,4096]{1,0:T(8,128)} %bitcast.3, s32[1,256]{1,0:T(1,128)} %len_hbm.1, s32[1,256]{1,0:T(1,128)} %reward_hbm.1, s32[1,256]{1,0:T(1,128)} %prompt_hbm.1), custom_call_target="tpu_custom_call" | custom-call | tf_op jit(solution)/shard_map/pallas_call | solution.py:314
  58.1 2.1 %shard_map.77 = (f32[16,16,4096]{2,1,0:T(8,128)}, f32[16,16]{1,0:T(8,128)}, f32[16,16]{1,0:T(8,128)}) custom-call(f32[16,16,4096]{2,1,0:T(8,128)S(1)} %get-tuple-element.6.grad, f32[16,16]{1,0:T(8,128)S(1)} %get-tuple-element.7.loss, f32[16,16]{1,0:T(8,128)S(1)} %get-tuple-element.8.adv), custom_call_target="tpu_custom_call" | custom-call | tf_op jit(solution)/shard_map/pallas_call | solution.py:349

commit v3 on v2

--- a/solution.py
+++ b/solution.py
@@ -20,7 +20,8 @@
 KL = 0.1
 LANES = 128
 UNIT = 256
-WIDTHS = (256, 512, 768, 1024, 1024, 512)
+BLOCK = 64
+WIDTHS = (512, 1024, 1536, 1024)
 STARTS = tuple(sum(WIDTHS[:i]) for i in range(len(WIDTHS)))
 CHUNKS = len(WIDTHS)
 
@@ -52,9 +53,10 @@
     policy_hbm, anchor_hbm, len_hbm, reward_hbm, prompt_hbm,
     grad_ref, loss_ref, adv_ref,
     policy, anchor, facts, stack, one_hot3, sent, got, sums, len_col,
-    info_out, info_in, sums_out, sums_in, count_out, count_in, len_in, adv_in,
+    info_out, info_in, sums_out, sums_in, count_out, count_in, total_out, total_in, len_in, adv_in,
     load_sem, facts_sem, send_sem, recv_sem,
     info_send, info_recv, sums_send, sums_recv, count_send, count_recv,
+    total_send, total_recv,
 ):
     mz, mc = lax.axis_index("gx_0"), lax.axis_index("gx_1")
     mx, my = lax.axis_index("gy_0"), lax.axis_index("gy_1")
@@ -79,65 +81,75 @@
         for i, source in enumerate((prompt_hbm, len_hbm, reward_hbm))
     ]
 
+    fact_loads[0].start()
+    for copy in loads(0):
+        copy.start()
     barrier = pltpu.get_barrier_semaphore()
     for dx, dy in OFFSETS:
         px, py = peer(dx, dy)
         pl.semaphore_signal(barrier, inc=1, device_id=(mz, mc, px, py), device_id_type=MESH)
-    for dz, dc in GX_OFFSETS:
-        pl.semaphore_signal(
-            barrier, inc=1, device_id=(lax.rem(mz + dz, 4), lax.rem(mc + dc, 2), mx, my), device_id_type=MESH
-        )
-    for copy in fact_loads:
+
+    @pl.when(me == 0)
+    def _():
+        for dz, dc in GX_OFFSETS:
+            pl.semaphore_signal(
+                barrier, inc=1, device_id=(lax.rem(mz + dz, 4), lax.rem(mc + dc, 2), mx, my), device_id_type=MESH
+            )
+
+    for copy in fact_loads[1:]:
         copy.start()
-    for ch in range(CHUNKS):
+    for ch in range(1, CHUNKS):
         for copy in loads(ch):
             copy.start()
-    for copy in fact_loads:
-        copy.wait()
+    fact_loads[0].wait()
 
     local_prompt = jnp.bitwise_and(facts[0], SLOTS - 1)
     rows = lax.broadcasted_iota(jnp.int32, (SLOTS, SLOTS), 0)
-    lanes = lax.broadcasted_iota(jnp.int32, (SLOTS, SLOTS), 1)
     hot = jnp.where(rows == local_prompt, 1.0, 0.0).astype(jnp.bfloat16)
     for part in range(3):
         one_hot3[:, part * SLOTS : (part + 1) * SLOTS] = hot
-    lens = facts[1].astype(jnp.float32)
-    column = jnp.sum(jnp.where(rows == lanes, lens, 0.0), axis=1, keepdims=True)
-    len_col[...] = jnp.broadcast_to(column, (SLOTS, LANES))
-    sums[...] = jnp.zeros_like(sums)
-
     def compute(ch):
         for copy in loads(ch):
             copy.wait()
 
-        @pl.loop(0, WIDTHS[ch] // UNIT)
-        def _(unit):
-            start = pl.multiple_of(STARTS[ch] + unit * UNIT, UNIT)
-
-            @pl.loop(0, SLOTS // 16)
+        unit = min(UNIT, WIDTHS[ch])
+
+        @pl.loop(0, WIDTHS[ch] // unit)
+        def _(step):
+            start = pl.multiple_of(STARTS[ch] + step * unit, unit)
+
+            @pl.loop(0, SLOTS // BLOCK)
             def _(block):
-                r0 = pl.multiple_of(block * 16, 16)
-                length = len_col[pl.ds(r0, 16), :]
-                s1 = sums[0, pl.ds(r0, 16), :]
-                s2 = sums[1, pl.ds(r0, 16), :]
-                lane = lax.broadcasted_iota(jnp.int32, (16, LANES), 1)
-                for t in range(UNIT // LANES):
-                    c0 = pl.multiple_of(start + t * LANES, LANES)
-                    p = policy[pl.ds(r0, 16), pl.ds(c0, LANES)]
-                    a = anchor[pl.ds(r0, 16), pl.ds(c0, LANES)]
-                    valid = (lane + c0).astype(jnp.float32) < length
-                    d = a - p
-                    ratio = jnp.exp(d)
-                    s1 = s1 + jnp.where(valid, p, 0.0)
-                    s2 = s2 + jnp.where(valid, ratio - d - 1.0, 0.0)
-                    for i, part in enumerate(parts_of(ratio)):
-                        stack[pl.ds(pl.multiple_of(i * SLOTS + r0, 16), 16), t * LANES : (t + 1) * LANES] = part
-                sums[0, pl.ds(r0, 16), :] = s1
-                sums[1, pl.ds(r0, 16), :] = s2
-
-            cols = pl.ds(start, UNIT)
-            sent[:, cols] = jnp.dot(one_hot3[...], stack[...], preferred_element_type=jnp.float32)
+                r0 = pl.multiple_of(block * BLOCK, BLOCK)
+                at, cols = pl.ds(r0, BLOCK), pl.ds(start, unit)
+                ratio = jnp.exp(anchor[at, cols] - policy[at, cols])
+                for i, part in enumerate(parts_of(ratio)):
+                    stack[pl.ds(pl.multiple_of(i * SLOTS + r0, BLOCK), BLOCK), 0:unit] = part
+
+            cols = pl.ds(start, unit)
+            sent[:, cols] = jnp.dot(one_hot3[...], stack[:, 0:unit], preferred_element_type=jnp.float32)
             got[me, :, cols] = sent[pl.ds(pl.multiple_of(me * 16, 16), 16), cols]
+
+    def add_sums(ch):
+        @pl.loop(0, SLOTS // 32)
+        def _(block):
+            at = pl.ds(pl.multiple_of(block * 32, 32), 32)
+            length = len_col[at, :]
+            lane = lax.broadcasted_iota(jnp.int32, (32, LANES), 1)
+
+            def add(t, so_far):
+                s1, s2 = so_far
+                c0 = pl.multiple_of(STARTS[ch] + t * LANES, LANES)
+                p = policy[at, pl.ds(c0, LANES)]
+                d = anchor[at, pl.ds(c0, LANES)] - p
+                valid = (lane + c0).astype(jnp.float32) < length
+                s1 = s1 + jnp.where(valid, p, 0.0)
+                s2 = s2 + jnp.where(valid, jnp.exp(d) - d - 1.0, 0.0)
+                return s1, s2
+
+            sums[0, at, :], sums[1, at, :] = lax.fori_loop(
+                0, WIDTHS[ch] // LANES, add, (sums[0, at, :], sums[1, at, :])
+            )
 
     def copies(ch):
         for j, (dx, dy) in enumerate(OFFSETS):
@@ -175,11 +187,50 @@
                 device_id_type=MESH,
             )
 
+    def total_copies():
+        for j, (dx, dy) in enumerate(OFFSETS):
+            px, py = peer(dx, dy)
+            yield pltpu.make_async_remote_copy(
+                src_ref=total_out,
+                dst_ref=total_in,
+                send_sem=total_send.at[j],
+                recv_sem=total_recv,
+                device_id=(mz, mc, px, py),
+                device_id_type=MESH,
+            )
+
+    def count_tokens():
+        info_in[me] = info_out[lax.div(mx, 2)]
+        for copy in small_copies(info_out, info_in, info_send, info_recv):
+            copy.wait_recv()
+
+        @pl.when(me == 0)
+        def _():
+            count = info_in[0, 2:3, :]
+            for k in range(1, MEMBERS):
+                count = count + info_in[k, 2:3, :]
+            count_out[...] = count
+            count_in[me_gx] = count
+            for copy in count_copies():
+                copy.start()
+            for copy in count_copies():
+                copy.wait_recv()
+            tokens = count_in[0]
+            for g in range(1, 8):
+                tokens = tokens + count_in[g]
+            total_out[...] = tokens
+            total_in[...] = tokens
+            for copy in total_copies():
+                copy.start()
+
     compute(0)
-    pl.semaphore_wait(barrier, len(OFFSETS) + len(GX_OFFSETS))
+    first = 1 - lax.min(me, 1)
+    pl.semaphore_wait(barrier, len(OFFSETS) + len(GX_OFFSETS) * first)
     for copy in copies(0):
         copy.start()
 
+    for copy in fact_loads[1:]:
+        copy.wait()
     hot = one_hot3[:, 0:SLOTS]
     lens = facts[1].astype(jnp.float32)
     rewards = facts[2].astype(jnp.float32) * 0.25
@@ -192,6 +243,11 @@
         info_out[half, 0:2, :] = moved[0:2, at : at + LANES]
         info_out[half, 2:4, :] = jnp.broadcast_to(local_count, (2, LANES))
 
+    lanes = lax.broadcasted_iota(jnp.int32, (SLOTS, SLOTS), 1)
+    column = jnp.sum(jnp.where(rows == lanes, lens, 0.0), axis=1, keepdims=True)
+    len_col[...] = jnp.broadcast_to(column, (SLOTS, LANES))
+    sums[...] = jnp.zeros_like(sums)
+
     compute(1)
     for copy in small_copies(info_out, info_in, info_send, info_recv):
         copy.start()
@@ -200,6 +256,8 @@
     for ch in range(2, CHUNKS):
         compute(ch)
         if ch == CHUNKS - 1:
+            for each in range(CHUNKS):
+                add_sums(each)
             ones = jnp.ones((8, LANES), jnp.float32)
             across = (((1,), (1,)), ((), ()))
             row1, row2 = (
@@ -216,19 +274,8 @@
                 copy.start()
         for copy in copies(ch):
             copy.start()
-
-    half = lax.div(mx, 2)
-    info_in[me] = info_out[half]
-    sums_in[me] = sums_out[half]
-    for copy in small_copies(info_out, info_in, info_send, info_recv):
-        copy.wait()
-    count = info_in[0, 2:3, :]
-    for k in range(1, MEMBERS):
-        count = count + info_in[k, 2:3, :]
-    count_out[...] = count
-    count_in[me_gx] = count
-    for copy in count_copies():
-        copy.start()
+        if ch == 2:
+            count_tokens()
 
     total = info_in[0, 1:2, :]
     for k in range(1, MEMBERS):
@@ -245,16 +292,17 @@
         len_in[k] = to_column(info_in[k, 0:1, :])
         adv_in[k] = to_column(advantage)
 
-    for copy in count_copies():
-        copy.wait()
-    tokens = count_in[0]
-    for g in range(1, 8):
-        tokens = tokens + count_in[g]
+    @pl.when(me != 0)
+    def _():
+        next(total_copies()).wait_recv()
+
+    tokens = total_in[...]
     grad_scale = SAMPLES * TOKENS / tokens
     loss_scale = SAMPLES / tokens
 
     for ch in range(CHUNKS):
         if ch == CHUNKS - 1:
+            sums_in[me] = sums_out[lax.div(mx, 2)]
             for copy in small_copies(sums_out, sums_in, sums_send, sums_recv):
                 copy.wait()
             member = lax.broadcasted_iota(jnp.int32, (MEMBERS, LANES), 0)
@@ -268,6 +316,14 @@
             select = jnp.where(mine, 1.0, 0.0).astype(jnp.bfloat16)
             loss_ref[...] = picked(loss_rows, select, 1)
             adv_ref[...] = picked(adv_rows, select, 1)
+            for copy in small_copies(info_out, info_in, info_send, info_recv):
+                copy.wait_send()
+
+            @pl.when(me == 0)
+            def _():
+                for copy in (*count_copies(), *total_copies()):
+                    copy.wait_send()
+
             for earlier in range(CHUNKS - 1):
                 for copy in copies(earlier):
                     copy.wait_send()
@@ -336,11 +392,14 @@
             pltpu.VMEM((MEMBERS, 2, LANES), f32),
             pltpu.VMEM((1, LANES), f32),
             pltpu.VMEM((8, 1, LANES), f32),
+            pltpu.VMEM((1, LANES), f32),
+            pltpu.VMEM((1, LANES), f32),
             pltpu.VMEM((MEMBERS, 16, LANES), f32),
             pltpu.VMEM((MEMBERS, 16, LANES), f32),
             dma((2, CHUNKS)), dma((3,)), dma((CHUNKS, n)), dma((CHUNKS, n)),
             dma((n,)), dma((n,)), dma((n,)), dma((n,)),
             dma((len(GX_OFFSETS),)), dma((len(GX_OFFSETS),)),
+            dma((n,)), dma,
         ],
         compiler_params=pltpu.CompilerParams(
             collective_id=0, has_side_effects=True, vmem_limit_bytes=50 * 2**20

time: 60.2 us -> 58.6 us (0.973)
  Pallas kernels: 59.5 us -> 57.5 us
    pallas_call x1, Pallas kernels: 57.4 us -> 55.4 us  [body(): pl.pallas_call(kernel, out_shape=(pltpu.VMEM((MEMBERS, 16, TOKENS), f32),...]
where the time goes in v3:
time: 58.6 us; the launch traced here: 58.2 us
  Pallas kernels  57.5 us (98%)
  between operations  0.64 us (1%)
    pallas_call x1, Pallas kernels, body(): pl.pallas_call(kernel, out_shape=(pltpu.VMEM((MEMBERS, 16, TOKENS), f32),...  55.4 us
    pallas_call x1, Pallas kernels, body(): pl.pallas_call(put_out, out_shape=(jax.ShapeDtypeStruct((MEMBERS, 16, TOK...  2.07 us

profile of v3, /device:TPU:0, one launch (start us, length us, event | category | flops | bytes accessed | tf_op | source)
XLA Modules:
  0.0 58.2 jit_solution(6813013883891547377)
XLA Ops:
  0.6 55.4 %shard_map.76 = (f32[16,16,4096]{2,1,0:T(8,128)S(1)}, f32[16,16]{1,0:T(8,128)S(1)}, f32[16,16]{1,0:T(8,128)S(1)}) custom-call(f32[256,4096]{1,0:T(8,128)} %bitcast.2, f32[256,4096]{1,0:T(8,128)} %bitcast.3, s32[1,256]{1,0:T(1,128)} %len_hbm.1, s32[1,256]{1,0:T(1,128)} %reward_hbm.1, s32[1,256]{1,0:T(1,128)} %prompt_hbm.1), custom_call_target="tpu_custom_call" | custom-call | tf_op jit(solution)/shard_map/pallas_call | solution.py:370
  56.1 2.1 %shard_map.77 = (f32[16,16,4096]{2,1,0:T(8,128)}, f32[16,16]{1,0:T(8,128)}, f32[16,16]{1,0:T(8,128)}) custom-call(f32[16,16,4096]{2,1,0:T(8,128)S(1)} %get-tuple-element.6.grad, f32[16,16]{1,0:T(8,128)S(1)} %get-tuple-element.7.loss, f32[16,16]{1,0:T(8,128)S(1)} %get-tuple-element.8.adv), custom_call_target="tpu_custom_call" | custom-call | tf_op jit(solution)/shard_map/pallas_call | solution.py:408

commit v4 on v3

--- a/solution.py
+++ b/solution.py
@@ -24,6 +24,7 @@
 WIDTHS = (512, 1024, 1536, 1024)
 STARTS = tuple(sum(WIDTHS[:i]) for i in range(len(WIDTHS)))
 CHUNKS = len(WIDTHS)
+LOADS = (WIDTHS[0] // 2, WIDTHS[0] // 2, *WIDTHS[1:])
 
 OFFSETS = (
     (2, 2), (2, 1), (1, 2), (2, 3), (3, 2), (1, 1), (3, 3), (1, 3),
@@ -69,11 +70,11 @@
     def columns(ch):
         return pl.ds(STARTS[ch], WIDTHS[ch])
 
-    def loads(ch):
-        cols = columns(ch)
+    def loads(part):
+        cols = pl.ds(sum(LOADS[:part]), LOADS[part])
         return (
-            pltpu.make_async_copy(policy_hbm.at[:, cols], policy.at[:, cols], load_sem.at[0, ch]),
-            pltpu.make_async_copy(anchor_hbm.at[:, cols], anchor.at[:, cols], load_sem.at[1, ch]),
+            pltpu.make_async_copy(policy_hbm.at[:, cols], policy.at[:, cols], load_sem.at[0, part]),
+            pltpu.make_async_copy(anchor_hbm.at[:, cols], anchor.at[:, cols], load_sem.at[1, part]),
         )
 
     fact_loads = [
@@ -98,8 +99,8 @@
 
     for copy in fact_loads[1:]:
         copy.start()
-    for ch in range(1, CHUNKS):
-        for copy in loads(ch):
+    for part in range(1, len(LOADS)):
+        for copy in loads(part):
             copy.start()
     fact_loads[0].wait()
 
@@ -108,23 +109,23 @@
     hot = jnp.where(rows == local_prompt, 1.0, 0.0).astype(jnp.bfloat16)
     for part in range(3):
         one_hot3[:, part * SLOTS : (part + 1) * SLOTS] = hot
-    def compute(ch):
-        for copy in loads(ch):
+    def compute(part):
+        for copy in loads(part):
             copy.wait()
 
-        unit = min(UNIT, WIDTHS[ch])
-
-        @pl.loop(0, WIDTHS[ch] // unit)
+        unit = min(UNIT, LOADS[part])
+
+        @pl.loop(0, LOADS[part] // unit)
         def _(step):
-            start = pl.multiple_of(STARTS[ch] + step * unit, unit)
+            start = pl.multiple_of(sum(LOADS[:part]) + step * unit, unit)
 
             @pl.loop(0, SLOTS // BLOCK)
             def _(block):
                 r0 = pl.multiple_of(block * BLOCK, BLOCK)
                 at, cols = pl.ds(r0, BLOCK), pl.ds(start, unit)
                 ratio = jnp.exp(anchor[at, cols] - policy[at, cols])
-                for i, part in enumerate(parts_of(ratio)):
-                    stack[pl.ds(pl.multiple_of(i * SLOTS + r0, BLOCK), BLOCK), 0:unit] = part
+                for i, piece in enumerate(parts_of(ratio)):
+                    stack[pl.ds(pl.multiple_of(i * SLOTS + r0, BLOCK), BLOCK), 0:unit] = piece
 
             cols = pl.ds(start, unit)
             sent[:, cols] = jnp.dot(one_hot3[...], stack[:, 0:unit], preferred_element_type=jnp.float32)
@@ -224,6 +225,7 @@
                 copy.start()
 
     compute(0)
+    compute(1)
     first = 1 - lax.min(me, 1)
     pl.semaphore_wait(barrier, len(OFFSETS) + len(GX_OFFSETS) * first)
     for copy in copies(0):
@@ -248,13 +250,13 @@
     len_col[...] = jnp.broadcast_to(column, (SLOTS, LANES))
     sums[...] = jnp.zeros_like(sums)
 
-    compute(1)
+    compute(2)
     for copy in small_copies(info_out, info_in, info_send, info_recv):
         copy.start()
     for copy in copies(1):
         copy.start()
     for ch in range(2, CHUNKS):
-        compute(ch)
+        compute(ch + 1)
         if ch == CHUNKS - 1:
             for each in range(CHUNKS):
                 add_sums(each)
@@ -327,11 +329,7 @@
             for earlier in range(CHUNKS - 1):
                 for copy in copies(earlier):
                     copy.wait_send()
-        for copy in copies(ch):
-            copy.wait_recv()
-
-        @pl.loop(0, MEMBERS)
-        def _(k):
+        def finish(k):
             length = len_in[k]
             advantage = adv_in[k]
             for t in range(WIDTHS[ch] // LANES):
@@ -341,6 +339,16 @@
                 grad_ref[k, :, c0 : c0 + LANES] = (
                     jnp.where(valid, KL * (1.0 - ratio) - advantage, 0.0) * grad_scale
                 )
+
+        if ch == CHUNKS - 1:
+            finish(me)
+            for copy, (dx, dy) in zip(copies(ch), OFFSETS):
+                copy.wait_recv()
+                finish(lax.rem(mx + 4 - dx, 4) * 4 + lax.rem(my + 4 - dy, 4))
+        else:
+            for copy in copies(ch):
+                copy.wait_recv()
+            pl.loop(0, MEMBERS)(finish)
 
     for copy in copies(CHUNKS - 1):
         copy.wait_send()
@@ -396,7 +404,7 @@
             pltpu.VMEM((1, LANES), f32),
             pltpu.VMEM((MEMBERS, 16, LANES), f32),
             pltpu.VMEM((MEMBERS, 16, LANES), f32),
-            dma((2, CHUNKS)), dma((3,)), dma((CHUNKS, n)), dma((CHUNKS, n)),
+            dma((2, len(LOADS))), dma((3,)), dma((CHUNKS, n)), dma((CHUNKS, n)),
             dma((n,)), dma((n,)), dma((n,)), dma((n,)),
             dma((len(GX_OFFSETS),)), dma((len(GX_OFFSETS),)),
             dma((n,)), dma,

time: 58.6 us -> 58.3 us (level)
  no operation moved by 1% of the time
where the time goes in v4:
time: 58.3 us; the launch traced here: 57.9 us
  Pallas kernels  57.3 us (98%)
  between operations  0.64 us (1%)
    pallas_call x1, Pallas kernels, body(): pl.pallas_call(kernel, out_shape=(pltpu.VMEM((MEMBERS, 16, TOKENS), f32),...  55.2 us
    pallas_call x1, Pallas kernels, body(): pl.pallas_call(put_out, out_shape=(jax.ShapeDtypeStruct((MEMBERS, 16, TOK...  2.07 us

profile of v4, /device:TPU:0, one launch (start us, length us, event | category | flops | bytes accessed | tf_op | source)
XLA Modules:
  0.0 57.9 jit_solution(9832628321025535087)
XLA Ops:
  0.6 55.2 %shard_map.76 = (f32[16,16,4096]{2,1,0:T(8,128)S(1)}, f32[16,16]{1,0:T(8,128)S(1)}, f32[16,16]{1,0:T(8,128)S(1)}) custom-call(f32[256,4096]{1,0:T(8,128)} %bitcast.2, f32[256,4096]{1,0:T(8,128)} %bitcast.3, s32[1,256]{1,0:T(1,128)} %len_hbm.1, s32[1,256]{1,0:T(1,128)} %reward_hbm.1, s32[1,256]{1,0:T(1,128)} %prompt_hbm.1), custom_call_target="tpu_custom_call" | custom-call | tf_op jit(solution)/shard_map/pallas_call | solution.py:378
  55.8 2.1 %shard_map.77 = (f32[16,16,4096]{2,1,0:T(8,128)}, f32[16,16]{1,0:T(8,128)}, f32[16,16]{1,0:T(8,128)}) custom-call(f32[16,16,4096]{2,1,0:T(8,128)S(1)} %get-tuple-element.6.grad, f32[16,16]{1,0:T(8,128)S(1)} %get-tuple-element.7.loss, f32[16,16]{1,0:T(8,128)S(1)} %get-tuple-element.8.adv), custom_call_target="tpu_custom_call" | custom-call | tf_op jit(solution)/shard_map/pallas_call | solution.py:416

commit v5 on v4

--- a/solution.py
+++ b/solution.py
@@ -20,7 +20,7 @@
 KL = 0.1
 LANES = 128
 UNIT = 256
-BLOCK = 64
+BLOCK = 128
 WIDTHS = (512, 1024, 1536, 1024)
 STARTS = tuple(sum(WIDTHS[:i]) for i in range(len(WIDTHS)))
 CHUNKS = len(WIDTHS)

time: 58.3 us -> 58.4 us (level)
  no operation moved by 1% of the time
where the time goes in v5:
time: 58.4 us; the launch traced here: 57.9 us
  Pallas kernels  57.3 us (98%)
  between operations  0.64 us (1%)
    pallas_call x1, Pallas kernels, body(): pl.pallas_call(kernel, out_shape=(pltpu.VMEM((MEMBERS, 16, TOKENS), f32),...  55.2 us
    pallas_call x1, Pallas kernels, body(): pl.pallas_call(put_out, out_shape=(jax.ShapeDtypeStruct((MEMBERS, 16, TOK...  2.07 us

profile of v5, /device:TPU:0, one launch (start us, length us, event | category | flops | bytes accessed | tf_op | source)
XLA Modules:
  0.0 57.9 jit_solution(12138514515435610937)
XLA Ops:
  0.6 55.2 %shard_map.76 = (f32[16,16,4096]{2,1,0:T(8,128)S(1)}, f32[16,16]{1,0:T(8,128)S(1)}, f32[16,16]{1,0:T(8,128)S(1)}) custom-call(f32[256,4096]{1,0:T(8,128)} %bitcast.2, f32[256,4096]{1,0:T(8,128)} %bitcast.3, s32[1,256]{1,0:T(1,128)} %len_hbm.1, s32[1,256]{1,0:T(1,128)} %reward_hbm.1, s32[1,256]{1,0:T(1,128)} %prompt_hbm.1), custom_call_target="tpu_custom_call" | custom-call | tf_op jit(solution)/shard_map/pallas_call | solution.py:378
  55.8 2.1 %shard_map.77 = (f32[16,16,4096]{2,1,0:T(8,128)}, f32[16,16]{1,0:T(8,128)}, f32[16,16]{1,0:T(8,128)}) custom-call(f32[16,16,4096]{2,1,0:T(8,128)S(1)} %get-tuple-element.6.grad, f32[16,16]{1,0:T(8,128)S(1)} %get-tuple-element.7.loss, f32[16,16]{1,0:T(8,128)S(1)} %get-tuple-element.8.adv), custom_call_target="tpu_custom_call" | custom-call | tf_op jit(solution)/shard_map/pallas_call | solution.py:416
